TPU v7x, 32 devices: a whole 2x2x4 slice. The times are simulated.
32 devices in a mesh: gx: 4 (over y, x), gy: 4 (over z), gz: 2 (over core).
Axes of the slice: x: 2, y: 2, z: 4, core: 2. Of those that a mesh axis runs over, the one named last changes fastest.
Arguments:
- right_side: float32 [64, 256, 1024], P('gx', 'gy', 'gz'), may hold values from -24 to 24
- reaction: float32 [64, 256, 1024], P('gx', 'gy', 'gz'), may hold values from 0.5 to 2
- velocity: float32 [3, 64, 256, 1024], P(None, 'gx', 'gy', 'gz'), may hold values from -0.5 to 0.5
Outputs:
- solution: float32 [64, 256, 1024], P('gx', 'gy', 'gz')
- residual: float32 [64, 256, 1024], P('gx', 'gy', 'gz')
- residual_norm: float32 [], replicated
All inputs are finite; a program needn't handle non-finite values.
Results may differ from a plain program's by a relative error of at most 0.00002.
Values sent between devices are 32-bit elements; how exact they have to be, the bound alone decides.
A program may use at most 128 MiB of HBM per device.

v0:
```python
import jax
import jax.numpy as jnp
from jax import lax
from jax.sharding import PartitionSpec as P

ITERS = 5


centre = 7.25
half_width = 6.75


def padded(cells, sides, width, closed):
    for axis, dim in sides:
        count = lax.axis_size(axis)
        ends = count if closed else count - 1
        head = lax.slice_in_dim(cells, 0, width, axis=dim)
        tail = lax.slice_in_dim(cells, cells.shape[dim] - width, cells.shape[dim], axis=dim)
        cells = jnp.concatenate(
            [
                lax.ppermute(tail, axis, [(i, (i + 1) % count) for i in range(ends)]),
                cells,
                lax.ppermute(head, axis, [((i + 1) % count, i) for i in range(ends)]),
            ],
            axis=dim,
        )
    return cells


def chebyshev_weights(count):
    ratio_value = centre / half_width
    weights = [1.0 / ratio_value]
    for iteration in range(count):
        weights.append(1.0 / (2.0 * ratio_value - weights[-1]))
    return weights


def combine(middle, plus_x, minus_x, plus_y, minus_y, plus_z, minus_z, reaction, velocity):
    beside = (1.0 - velocity[0]) * plus_x + (1.0 + velocity[0]) * minus_x
    beside = beside + (1.0 - velocity[1]) * plus_y + (1.0 + velocity[1]) * minus_y
    beside = beside + (1.0 - velocity[2]) * plus_z + (1.0 + velocity[2]) * minus_z
    return (6.0 + reaction) * middle - beside


def apply_single(values, reaction, velocity):
    wrapped = padded(values, (("gx", 0),), 1, True)
    opened = padded(values, (("gy", 1), ("gz", 2)), 1, False)
    return combine(
        values,
        wrapped[2:],
        wrapped[:-2],
        opened[:, 2:, 1:-1],
        opened[:, :-2, 1:-1],
        opened[:, 1:-1, 2:],
        opened[:, 1:-1, :-2],
        reaction,
        velocity,
    )


def local(right_side, reaction, velocity):
    weights = chebyshev_weights(ITERS)
    solution = jnp.zeros_like(right_side)
    residual = right_side
    direction = right_side / centre
    for iteration in range(ITERS):
        applied = apply_single(direction, reaction, velocity)
        solution = solution + direction
        residual = residual - applied
        if iteration + 1 < ITERS:
            direction = (
                weights[iteration + 1] * weights[iteration] * direction
                + 2.0 * weights[iteration + 1] / half_width * residual
            )
    local_sum = jnp.sum(residual * residual)
    total = lax.psum(local_sum, ("gx", "gy", "gz"))
    cells_all = (
        residual.shape[0]
        * residual.shape[1]
        * residual.shape[2]
        * lax.axis_size("gx")
        * lax.axis_size("gy")
        * lax.axis_size("gz")
    )
    residual_norm = jnp.sqrt(total / cells_all + 1e-06)
    return (solution, residual, residual_norm)


def solution(mesh):
    return jax.shard_map(
        local,
        mesh=mesh,
        in_specs=(P("gx", "gy", "gz"), P("gx", "gy", "gz"), P(None, "gx", "gy", "gz")),
        out_specs=(P("gx", "gy", "gz"), P("gx", "gy", "gz"), P()),
        check_vma=False,
    )
```

profile of v0, /device:TPU:0, one launch (start us, length us, event | category | flops | bytes accessed | tf_op | source)
XLA Modules:
  0.0 192.9 jit_solution(8272667532759159386)
XLA Ops:
  0.6 1.8 broadcast_multiply_fusion
  2.6 1.3 collective-permute-start.2
  3.9 5.6 %collective-permute-start.3 = (f32[16,1,512]{2,0,1:T(8,128)S(1)}, f32[16,1,512]{2,0,1:T(8,128)S(1)}, u32[]{:S(2)}, u32[]{:S(2)}) collective-permute-start(f32[16,1,512]{2,0,1:T(8,128)S(1)} %copy.17), channel_id=1, source_target_pairs={{0,2},{2,4},{4,6},{1,3},{3,5},{5,7},{8,10},{10,12},{12,14},{9,11},... | collective-permute-start | bytes 98312 | tf_op jit(solution)/shard_map/ppermute | solution.py:21
  9.5 0.7 fusion.78
  10.2 2.9 %collective-permute-start = (f32[1,64,512]{2,1,0:T(8,128)}, f32[1,64,512]{2,1,0:T(8,128)S(1)}, u32[]{:S(2)}, u32[]{:S(2)}) collective-permute-start(f32[1,64,512]{2,1,0:T(8,128)} %get-tuple-element.42), channel_id=1, source_target_pairs={{8,0},{16,8},{24,16},{0,24},{9,1},{17,9},{25,17},{1,25},{10,2},{18... | collective-permute-start | bytes 393224 | tf_op jit(solution)/shard_map/ppermute | solution.py:23
  13.7 1.4 collective-permute-start.4
  15.4 3.0 %collective-permute-start.5 = (f32[16,66,1]{1,0,2:T(8,128)S(1)}, f32[16,66,1]{1,0,2:T(8,128)S(1)}, u32[]{:S(2)}, u32[]{:S(2)}) collective-permute-start(f32[16,66,1]{1,0,2:T(8,128)S(1)} %copy.23), channel_id=1, source_target_pairs={{0,1},{2,3},{4,5},{6,7},{8,9},{10,11},{12,13},{14,15},{16,17},{18,... | collective-permute-start | bytes 12680 | tf_op jit(solution)/shard_map/ppermute | solution.py:21
  18.4 0.3 copy.22
  18.7 0.5 collective-permute-done.5
  19.2 0.3 copy.24
  19.7 12.0 %multiply_add_fusion.3 = (f32[16,64,512]{2,1,0:T(8,128)S(1)}, f32[16,64,512]{2,1,0:T(8,128)}) fusion(f32[16,64,512]{2,1,0:T(8,128)} %param.3, f32[16,1,512]{2,1,0:T(1,128)S(1)} %copy.16, f32[16,64,512]{2,1,0:T(8,128)} %copy-done.5, f32[16,1,512]{2,1,0:T(1,128)S(1)} %copy.18, f32[16,66,1]{2,1,0:T(8,128)S(1)} %copy.24, f32[16,66,1]{2,1,0:T(8,128)S(1)} %copy.22, ...), kind=kLoop, calls=%fused_computation.120 | loop fusion | flops 17825792 | bytes 17113344 | tf_op jit(solution)/shard_map/add | solution.py:72
  31.8 1.3 collective-permute-start.8
  33.1 4.5 %collective-permute-start.9 = (f32[16,1,512]{2,0,1:T(8,128)S(1)}, f32[16,1,512]{2,0,1:T(8,128)S(1)}, u32[]{:S(2)}, u32[]{:S(2)}) collective-permute-start(f32[16,1,512]{2,0,1:T(8,128)S(1)} %copy.27), channel_id=1, source_target_pairs={{0,2},{2,4},{4,6},{1,3},{3,5},{5,7},{8,10},{10,12},{12,14},{9,11},... | collective-permute-start | bytes 98312 | tf_op jit(solution)/shard_map/ppermute | solution.py:21
  37.6 0.7 fusion.76
  38.3 2.8 %collective-permute-start.6 = (f32[1,64,512]{2,1,0:T(8,128)}, f32[1,64,512]{2,1,0:T(8,128)S(1)}, u32[]{:S(2)}, u32[]{:S(2)}) collective-permute-start(f32[1,64,512]{2,1,0:T(8,128)} %get-tuple-element.38), channel_id=1, source_target_pairs={{8,0},{16,8},{24,16},{0,24},{9,1},{17,9},{25,17},{1,25},{10,2},{18... | collective-permute-start | bytes 393224 | tf_op jit(solution)/shard_map/ppermute | solution.py:23
  41.8 1.3 collective-permute-start.10
  43.4 3.0 %collective-permute-start.11 = (f32[16,66,1]{1,0,2:T(8,128)S(1)}, f32[16,66,1]{1,0,2:T(8,128)S(1)}, u32[]{:S(2)}, u32[]{:S(2)}) collective-permute-start(f32[16,66,1]{1,0,2:T(8,128)S(1)} %copy.33), channel_id=1, source_target_pairs={{0,1},{2,3},{4,5},{6,7},{8,9},{10,11},{12,13},{14,15},{16,17},{18,... | collective-permute-start | bytes 12680 | tf_op jit(solution)/shard_map/ppermute | solution.py:21
  46.4 0.3 copy.32
  46.7 0.5 collective-permute-done.11
  47.7 12.4 %multiply_add_fusion.2 = (f32[16,64,512]{2,1,0:T(8,128)S(1)}, f32[16,64,512]{2,1,0:T(8,128)}) fusion(f32[16,64,512]{2,1,0:T(8,128)} %copy-done.1, f32[16,64,512]{2,1,0:T(8,128)} %get-tuple-element.15, f32[16,1,512]{2,1,0:T(1,128)S(1)} %copy.26, f32[16,1,512]{2,1,0:T(1,128)S(1)} %copy.28, f32[16,66,1]{2,1,0:T(8,128)S(1)} %copy.34, ...), kind=kLoop, calls=%fused_computation.119 | loop fusion | flops 17825792 | bytes 17113344 | tf_op jit(solution)/shard_map/add | solution.py:72
  60.2 1.3 collective-permute-start.14
  61.5 4.5 %collective-permute-start.15 = (f32[16,1,512]{2,0,1:T(8,128)S(1)}, f32[16,1,512]{2,0,1:T(8,128)S(1)}, u32[]{:S(2)}, u32[]{:S(2)}) collective-permute-start(f32[16,1,512]{2,0,1:T(8,128)S(1)} %copy.37), channel_id=1, source_target_pairs={{0,2},{2,4},{4,6},{1,3},{3,5},{5,7},{8,10},{10,12},{12,14},{9,11},... | collective-permute-start | bytes 98312 | tf_op jit(solution)/shard_map/ppermute | solution.py:21
  66.1 0.7 fusion.74
  66.8 2.7 %collective-permute-start.12 = (f32[1,64,512]{2,1,0:T(8,128)}, f32[1,64,512]{2,1,0:T(8,128)S(1)}, u32[]{:S(2)}, u32[]{:S(2)}) collective-permute-start(f32[1,64,512]{2,1,0:T(8,128)} %get-tuple-element.34), channel_id=1, source_target_pairs={{8,0},{16,8},{24,16},{0,24},{9,1},{17,9},{25,17},{1,25},{10,2},{18... | collective-permute-start | bytes 393224 | tf_op jit(solution)/shard_map/ppermute | solution.py:23
  70.1 1.3 collective-permute-start.16
  71.7 3.0 %collective-permute-start.17 = (f32[16,66,1]{1,0,2:T(8,128)S(1)}, f32[16,66,1]{1,0,2:T(8,128)S(1)}, u32[]{:S(2)}, u32[]{:S(2)}) collective-permute-start(f32[16,66,1]{1,0,2:T(8,128)S(1)} %copy.43), channel_id=1, source_target_pairs={{0,1},{2,3},{4,5},{6,7},{8,9},{10,11},{12,13},{14,15},{16,17},{18,... | collective-permute-start | bytes 12680 | tf_op jit(solution)/shard_map/ppermute | solution.py:21
  74.7 0.3 copy.42
  75.1 0.5 collective-permute-done.17
  76.1 12.7 %multiply_add_fusion.1 = (f32[16,64,512]{2,1,0:T(8,128)S(1)}, f32[16,64,512]{2,1,0:T(8,128)}) fusion(f32[16,64,512]{2,1,0:T(8,128)} %copy-done.2, f32[16,64,512]{2,1,0:T(8,128)} %get-tuple-element.13, f32[16,1,512]{2,1,0:T(1,128)S(1)} %copy.36, f32[16,1,512]{2,1,0:T(1,128)S(1)} %copy.38, f32[16,66,1]{2,1,0:T(8,128)S(1)} %copy.44, ...), kind=kLoop, calls=%fused_computation.118 | loop fusion | flops 17825792 | bytes 17113344 | tf_op jit(solution)/shard_map/add | solution.py:72
  88.9 1.3 collective-permute-start.20
  90.2 4.5 %collective-permute-start.21 = (f32[16,1,512]{2,0,1:T(8,128)S(1)}, f32[16,1,512]{2,0,1:T(8,128)S(1)}, u32[]{:S(2)}, u32[]{:S(2)}) collective-permute-start(f32[16,1,512]{2,0,1:T(8,128)S(1)} %copy.47), channel_id=1, source_target_pairs={{0,2},{2,4},{4,6},{1,3},{3,5},{5,7},{8,10},{10,12},{12,14},{9,11},... | collective-permute-start | bytes 98312 | tf_op jit(solution)/shard_map/ppermute | solution.py:21
  94.7 0.7 fusion.72
  95.5 2.7 %collective-permute-start.18 = (f32[1,64,512]{2,1,0:T(8,128)}, f32[1,64,512]{2,1,0:T(8,128)S(1)}, u32[]{:S(2)}, u32[]{:S(2)}) collective-permute-start(f32[1,64,512]{2,1,0:T(8,128)} %get-tuple-element.30), channel_id=1, source_target_pairs={{8,0},{16,8},{24,16},{0,24},{9,1},{17,9},{25,17},{1,25},{10,2},{18... | collective-permute-start | bytes 393224 | tf_op jit(solution)/shard_map/ppermute | solution.py:23
  98.8 1.4 collective-permute-start.22
  100.5 3.0 %collective-permute-start.23 = (f32[16,66,1]{1,0,2:T(8,128)S(1)}, f32[16,66,1]{1,0,2:T(8,128)S(1)}, u32[]{:S(2)}, u32[]{:S(2)}) collective-permute-start(f32[16,66,1]{1,0,2:T(8,128)S(1)} %copy.53), channel_id=1, source_target_pairs={{0,1},{2,3},{4,5},{6,7},{8,9},{10,11},{12,13},{14,15},{16,17},{18,... | collective-permute-start | bytes 12680 | tf_op jit(solution)/shard_map/ppermute | solution.py:21
  103.6 0.3 copy.52
  103.9 0.5 collective-permute-done.23
  104.8 12.2 %multiply_add_fusion = (f32[16,64,512]{2,1,0:T(8,128)S(1)}, f32[16,64,512]{2,1,0:T(8,128)}) fusion(f32[16,64,512]{2,1,0:T(8,128)} %copy-done.3, f32[16,64,512]{2,1,0:T(8,128)} %get-tuple-element.11, f32[16,1,512]{2,1,0:T(1,128)S(1)} %copy.46, f32[16,1,512]{2,1,0:T(1,128)S(1)} %copy.48, f32[16,66,1]{2,1,0:T(8,128)S(1)} %copy.54, f32[16,66,1]{2,1,0:T(8,128)S(1)} %copy.52, ...), kind=kLoop, calls=%fused_computation.116 | loop fusion | flops 17825792 | bytes 17113344 | tf_op jit(solution)/shard_map/add | solution.py:72
  117.1 1.3 collective-permute-start.26
  118.4 4.5 %collective-permute-start.27 = (f32[16,1,512]{2,0,1:T(8,128)S(1)}, f32[16,1,512]{2,0,1:T(8,128)S(1)}, u32[]{:S(2)}, u32[]{:S(2)}) collective-permute-start(f32[16,1,512]{2,0,1:T(8,128)S(1)} %copy.57), channel_id=1, source_target_pairs={{0,2},{2,4},{4,6},{1,3},{3,5},{5,7},{8,10},{10,12},{12,14},{9,11},... | collective-permute-start | bytes 98312 | tf_op jit(solution)/shard_map/ppermute | solution.py:21
  123.0 0.7 fusion.70
  123.7 2.9 %collective-permute-start.24 = (f32[1,64,512]{2,1,0:T(8,128)}, f32[1,64,512]{2,1,0:T(8,128)S(1)}, u32[]{:S(2)}, u32[]{:S(2)}) collective-permute-start(f32[1,64,512]{2,1,0:T(8,128)} %get-tuple-element.26), channel_id=1, source_target_pairs={{8,0},{16,8},{24,16},{0,24},{9,1},{17,9},{25,17},{1,25},{10,2},{18... | collective-permute-start | bytes 393224 | tf_op jit(solution)/shard_map/ppermute | solution.py:23
  127.4 1.4 collective-permute-start.29
  128.9 1.3 collective-permute-start.28
  130.2 6.8 %add_add_fusion = f32[16,64,512]{2,1,0:T(8,128)} fusion(f32[16,64,512]{2,1,0:T(8,128)} %copy-done.3, f32[16,64,512]{2,1,0:T(8,128)} %copy-done.2, f32[16,64,512]{2,1,0:T(8,128)} %copy-done.1, f32[16,64,512]{2,1,0:T(8,128)} %get-tuple-element.9, f32[16,64,512]{2,1,0:T(8,128)} %param.3), kind=kLoop, calls=%fused_computation.117 | loop fusion | flops 4194304 | bytes 12582912 | tf_op jit(solution)/shard_map/add | solution.py:68
  137.3 0.3 copy.64
  137.6 12.5 %multiply_reduce_fusion = (f32[]{:T(128)}, f32[16,64,512]{2,1,0:T(8,128)}) fusion(f32[16,64,512]{2,1,0:T(8,128)} %get-tuple-element.9, f32[16,1,512]{2,1,0:T(1,128)S(1)} %copy.56, f32[16,64,512]{2,1,0:T(8,128)} %copy-done.4, f32[16,1,512]{2,1,0:T(1,128)S(1)} %copy.58, f32[16,66,1]{2,1,0:T(8,128)S(1)} %copy.64, f32[16,66,1]{2,1,0:T(8,128)S(1)} %copy.62, ...), kind=kLoop, calls=%fused_computation.115 | loop fusion | flops 17301504 | bytes 15016196 | tf_op jit(solution)/shard_map/reduce_sum | solution.py:75
  150.1 41.0 %psum.7 = f32[]{:T(128)} all-reduce(f32[]{:T(128)} %get-tuple-element.6), channel_id=1, replica_groups=mesh['gx'=4,'gy'=4,'gz'=2] {'gx','gy','gz'}, use_global_device_ids=true, to_apply=%region_1.0 | all-reduce | flops 1 | bytes 8 | tf_op jit(solution)/shard_map/psum | solution.py:76
  (87 shorter events, 6.4 us)
Async XLA Ops:
  2.5 11.0 %copy-start.5 = (f32[16,64,512]{2,1,0:T(8,128)}, f32[16,64,512]{2,1,0:T(8,128)S(1)}, u32[]{:S(2)}) copy-start(f32[16,64,512]{2,1,0:T(8,128)S(1)} %broadcast_multiply_fusion) | copy-start | bytes 6291460
  2.6 10.5 %collective-permute-start.2 = (f32[16,1,512]{2,0,1:T(8,128)S(1)}, f32[16,1,512]{2,0,1:T(8,128)S(1)}, u32[]{:S(2)}, u32[]{:S(2)}) collective-permute-start(f32[16,1,512]{2,0,1:T(8,128)S(1)} %copy.15), channel_id=1, source_target_pairs={{2,0},{4,2},{6,4},{3,1},{5,3},{7,5},{10,8},{12,10},{14,12},{11,9},... | collective-permute-start | bytes 98312 | tf_op jit(solution)/shard_map/ppermute | solution.py:23
  3.9 9.2 %collective-permute-start.3 = (f32[16,1,512]{2,0,1:T(8,128)S(1)}, f32[16,1,512]{2,0,1:T(8,128)S(1)}, u32[]{:S(2)}, u32[]{:S(2)}) collective-permute-start(f32[16,1,512]{2,0,1:T(8,128)S(1)} %copy.17), channel_id=1, source_target_pairs={{0,2},{2,4},{4,6},{1,3},{3,5},{5,7},{8,10},{10,12},{12,14},{9,11},... | collective-permute-start | bytes 98312 | tf_op jit(solution)/shard_map/ppermute | solution.py:21
  10.2 9.4 %collective-permute-start = (f32[1,64,512]{2,1,0:T(8,128)}, f32[1,64,512]{2,1,0:T(8,128)S(1)}, u32[]{:S(2)}, u32[]{:S(2)}) collective-permute-start(f32[1,64,512]{2,1,0:T(8,128)} %get-tuple-element.42), channel_id=1, source_target_pairs={{8,0},{16,8},{24,16},{0,24},{9,1},{17,9},{25,17},{1,25},{10,2},{18... | collective-permute-start | bytes 393224 | tf_op jit(solution)/shard_map/ppermute | solution.py:23
  13.1 6.6 %collective-permute-start.1 = (f32[1,64,512]{2,1,0:T(8,128)}, f32[1,64,512]{2,1,0:T(8,128)}, u32[]{:S(2)}, u32[]{:S(2)}) collective-permute-start(f32[1,64,512]{2,1,0:T(8,128)} %get-tuple-element.43), channel_id=1, source_target_pairs={{0,8},{8,16},{16,24},{24,0},{1,9},{9,17},{17,25},{25,1},{2,10},{10... | collective-permute-start | bytes 393224 | tf_op jit(solution)/shard_map/ppermute | solution.py:21
  13.2 6.5 %copy-start = (f32[16,64,512]{2,1,0:T(8,128)S(1)}, f32[16,64,512]{2,1,0:T(8,128)}, u32[]{:S(2)}) copy-start(f32[16,64,512]{2,1,0:T(8,128)} %param.4) | copy-start | bytes 6291460
  13.7 4.7 %collective-permute-start.4 = (f32[16,66,1]{1,0,2:T(8,128)S(1)}, f32[16,66,1]{1,0,2:T(8,128)S(1)}, u32[]{:S(2)}, u32[]{:S(2)}) collective-permute-start(f32[16,66,1]{1,0,2:T(8,128)S(1)} %copy.21), channel_id=1, source_target_pairs={{1,0},{3,2},{5,4},{7,6},{9,8},{11,10},{13,12},{15,14},{17,16},{19,... | collective-permute-start | bytes 12680 | tf_op jit(solution)/shard_map/ppermute | solution.py:23
  15.4 3.9 %collective-permute-start.5 = (f32[16,66,1]{1,0,2:T(8,128)S(1)}, f32[16,66,1]{1,0,2:T(8,128)S(1)}, u32[]{:S(2)}, u32[]{:S(2)}) collective-permute-start(f32[16,66,1]{1,0,2:T(8,128)S(1)} %copy.23), channel_id=1, source_target_pairs={{0,1},{2,3},{4,5},{6,7},{8,9},{10,11},{12,13},{14,15},{16,17},{18,... | collective-permute-start | bytes 12680 | tf_op jit(solution)/shard_map/ppermute | solution.py:21
  31.7 9.9 %copy-start.1 = (f32[16,64,512]{2,1,0:T(8,128)}, f32[16,64,512]{2,1,0:T(8,128)S(1)}, u32[]{:S(2)}) copy-start(f32[16,64,512]{2,1,0:T(8,128)S(1)} %get-tuple-element.14) | copy-start | bytes 6291460
  31.8 9.4 %collective-permute-start.8 = (f32[16,1,512]{2,0,1:T(8,128)S(1)}, f32[16,1,512]{2,0,1:T(8,128)S(1)}, u32[]{:S(2)}, u32[]{:S(2)}) collective-permute-start(f32[16,1,512]{2,0,1:T(8,128)S(1)} %copy.25), channel_id=1, source_target_pairs={{2,0},{4,2},{6,4},{3,1},{5,3},{7,5},{10,8},{12,10},{14,12},{11,9},... | collective-permute-start | bytes 98312 | tf_op jit(solution)/shard_map/ppermute | solution.py:23
  33.1 8.2 %collective-permute-start.9 = (f32[16,1,512]{2,0,1:T(8,128)S(1)}, f32[16,1,512]{2,0,1:T(8,128)S(1)}, u32[]{:S(2)}, u32[]{:S(2)}) collective-permute-start(f32[16,1,512]{2,0,1:T(8,128)S(1)} %copy.27), channel_id=1, source_target_pairs={{0,2},{2,4},{4,6},{1,3},{3,5},{5,7},{8,10},{10,12},{12,14},{9,11},... | collective-permute-start | bytes 98312 | tf_op jit(solution)/shard_map/ppermute | solution.py:21
  38.3 9.2 %collective-permute-start.6 = (f32[1,64,512]{2,1,0:T(8,128)}, f32[1,64,512]{2,1,0:T(8,128)S(1)}, u32[]{:S(2)}, u32[]{:S(2)}) collective-permute-start(f32[1,64,512]{2,1,0:T(8,128)} %get-tuple-element.38), channel_id=1, source_target_pairs={{8,0},{16,8},{24,16},{0,24},{9,1},{17,9},{25,17},{1,25},{10,2},{18... | collective-permute-start | bytes 393224 | tf_op jit(solution)/shard_map/ppermute | solution.py:23
  41.2 6.6 %collective-permute-start.7 = (f32[1,64,512]{2,1,0:T(8,128)}, f32[1,64,512]{2,1,0:T(8,128)}, u32[]{:S(2)}, u32[]{:S(2)}) collective-permute-start(f32[1,64,512]{2,1,0:T(8,128)} %get-tuple-element.39), channel_id=1, source_target_pairs={{0,8},{8,16},{16,24},{24,0},{1,9},{9,17},{17,25},{25,1},{2,10},{10... | collective-permute-start | bytes 393224 | tf_op jit(solution)/shard_map/ppermute | solution.py:21
  41.8 4.6 %collective-permute-start.10 = (f32[16,66,1]{1,0,2:T(8,128)S(1)}, f32[16,66,1]{1,0,2:T(8,128)S(1)}, u32[]{:S(2)}, u32[]{:S(2)}) collective-permute-start(f32[16,66,1]{1,0,2:T(8,128)S(1)} %copy.31), channel_id=1, source_target_pairs={{1,0},{3,2},{5,4},{7,6},{9,8},{11,10},{13,12},{15,14},{17,16},{19,... | collective-permute-start | bytes 12680 | tf_op jit(solution)/shard_map/ppermute | solution.py:23
  43.4 3.9 %collective-permute-start.11 = (f32[16,66,1]{1,0,2:T(8,128)S(1)}, f32[16,66,1]{1,0,2:T(8,128)S(1)}, u32[]{:S(2)}, u32[]{:S(2)}) collective-permute-start(f32[16,66,1]{1,0,2:T(8,128)S(1)} %copy.33), channel_id=1, source_target_pairs={{0,1},{2,3},{4,5},{6,7},{8,9},{10,11},{12,13},{14,15},{16,17},{18,... | collective-permute-start | bytes 12680 | tf_op jit(solution)/shard_map/ppermute | solution.py:21
  60.1 9.8 %copy-start.2 = (f32[16,64,512]{2,1,0:T(8,128)}, f32[16,64,512]{2,1,0:T(8,128)S(1)}, u32[]{:S(2)}) copy-start(f32[16,64,512]{2,1,0:T(8,128)S(1)} %get-tuple-element.12) | copy-start | bytes 6291460
  60.2 9.3 %collective-permute-start.14 = (f32[16,1,512]{2,0,1:T(8,128)S(1)}, f32[16,1,512]{2,0,1:T(8,128)S(1)}, u32[]{:S(2)}, u32[]{:S(2)}) collective-permute-start(f32[16,1,512]{2,0,1:T(8,128)S(1)} %copy.35), channel_id=1, source_target_pairs={{2,0},{4,2},{6,4},{3,1},{5,3},{7,5},{10,8},{12,10},{14,12},{11,9},... | collective-permute-start | bytes 98312 | tf_op jit(solution)/shard_map/ppermute | solution.py:23
  61.5 8.1 %collective-permute-start.15 = (f32[16,1,512]{2,0,1:T(8,128)S(1)}, f32[16,1,512]{2,0,1:T(8,128)S(1)}, u32[]{:S(2)}, u32[]{:S(2)}) collective-permute-start(f32[16,1,512]{2,0,1:T(8,128)S(1)} %copy.37), channel_id=1, source_target_pairs={{0,2},{2,4},{4,6},{1,3},{3,5},{5,7},{8,10},{10,12},{12,14},{9,11},... | collective-permute-start | bytes 98312 | tf_op jit(solution)/shard_map/ppermute | solution.py:21
  66.8 9.1 %collective-permute-start.12 = (f32[1,64,512]{2,1,0:T(8,128)}, f32[1,64,512]{2,1,0:T(8,128)S(1)}, u32[]{:S(2)}, u32[]{:S(2)}) collective-permute-start(f32[1,64,512]{2,1,0:T(8,128)} %get-tuple-element.34), channel_id=1, source_target_pairs={{8,0},{16,8},{24,16},{0,24},{9,1},{17,9},{25,17},{1,25},{10,2},{18... | collective-permute-start | bytes 393224 | tf_op jit(solution)/shard_map/ppermute | solution.py:23
  69.5 6.6 %collective-permute-start.13 = (f32[1,64,512]{2,1,0:T(8,128)}, f32[1,64,512]{2,1,0:T(8,128)}, u32[]{:S(2)}, u32[]{:S(2)}) collective-permute-start(f32[1,64,512]{2,1,0:T(8,128)} %get-tuple-element.35), channel_id=1, source_target_pairs={{0,8},{8,16},{16,24},{24,0},{1,9},{9,17},{17,25},{25,1},{2,10},{10... | collective-permute-start | bytes 393224 | tf_op jit(solution)/shard_map/ppermute | solution.py:21
  70.1 4.6 %collective-permute-start.16 = (f32[16,66,1]{1,0,2:T(8,128)S(1)}, f32[16,66,1]{1,0,2:T(8,128)S(1)}, u32[]{:S(2)}, u32[]{:S(2)}) collective-permute-start(f32[16,66,1]{1,0,2:T(8,128)S(1)} %copy.41), channel_id=1, source_target_pairs={{1,0},{3,2},{5,4},{7,6},{9,8},{11,10},{13,12},{15,14},{17,16},{19,... | collective-permute-start | bytes 12680 | tf_op jit(solution)/shard_map/ppermute | solution.py:23
  71.7 3.9 %collective-permute-start.17 = (f32[16,66,1]{1,0,2:T(8,128)S(1)}, f32[16,66,1]{1,0,2:T(8,128)S(1)}, u32[]{:S(2)}, u32[]{:S(2)}) collective-permute-start(f32[16,66,1]{1,0,2:T(8,128)S(1)} %copy.43), channel_id=1, source_target_pairs={{0,1},{2,3},{4,5},{6,7},{8,9},{10,11},{12,13},{14,15},{16,17},{18,... | collective-permute-start | bytes 12680 | tf_op jit(solution)/shard_map/ppermute | solution.py:21
  88.8 9.8 %copy-start.3 = (f32[16,64,512]{2,1,0:T(8,128)}, f32[16,64,512]{2,1,0:T(8,128)S(1)}, u32[]{:S(2)}) copy-start(f32[16,64,512]{2,1,0:T(8,128)S(1)} %get-tuple-element.10) | copy-start | bytes 6291460
  88.9 9.3 %collective-permute-start.20 = (f32[16,1,512]{2,0,1:T(8,128)S(1)}, f32[16,1,512]{2,0,1:T(8,128)S(1)}, u32[]{:S(2)}, u32[]{:S(2)}) collective-permute-start(f32[16,1,512]{2,0,1:T(8,128)S(1)} %copy.45), channel_id=1, source_target_pairs={{2,0},{4,2},{6,4},{3,1},{5,3},{7,5},{10,8},{12,10},{14,12},{11,9},... | collective-permute-start | bytes 98312 | tf_op jit(solution)/shard_map/ppermute | solution.py:23
  90.2 8.0 %collective-permute-start.21 = (f32[16,1,512]{2,0,1:T(8,128)S(1)}, f32[16,1,512]{2,0,1:T(8,128)S(1)}, u32[]{:S(2)}, u32[]{:S(2)}) collective-permute-start(f32[16,1,512]{2,0,1:T(8,128)S(1)} %copy.47), channel_id=1, source_target_pairs={{0,2},{2,4},{4,6},{1,3},{3,5},{5,7},{8,10},{10,12},{12,14},{9,11},... | collective-permute-start | bytes 98312 | tf_op jit(solution)/shard_map/ppermute | solution.py:21
  95.5 9.2 %collective-permute-start.18 = (f32[1,64,512]{2,1,0:T(8,128)}, f32[1,64,512]{2,1,0:T(8,128)S(1)}, u32[]{:S(2)}, u32[]{:S(2)}) collective-permute-start(f32[1,64,512]{2,1,0:T(8,128)} %get-tuple-element.30), channel_id=1, source_target_pairs={{8,0},{16,8},{24,16},{0,24},{9,1},{17,9},{25,17},{1,25},{10,2},{18... | collective-permute-start | bytes 393224 | tf_op jit(solution)/shard_map/ppermute | solution.py:23
  98.2 6.6 %collective-permute-start.19 = (f32[1,64,512]{2,1,0:T(8,128)}, f32[1,64,512]{2,1,0:T(8,128)}, u32[]{:S(2)}, u32[]{:S(2)}) collective-permute-start(f32[1,64,512]{2,1,0:T(8,128)} %get-tuple-element.31), channel_id=1, source_target_pairs={{0,8},{8,16},{16,24},{24,0},{1,9},{9,17},{17,25},{25,1},{2,10},{10... | collective-permute-start | bytes 393224 | tf_op jit(solution)/shard_map/ppermute | solution.py:21
  98.8 4.7 %collective-permute-start.22 = (f32[16,66,1]{1,0,2:T(8,128)S(1)}, f32[16,66,1]{1,0,2:T(8,128)S(1)}, u32[]{:S(2)}, u32[]{:S(2)}) collective-permute-start(f32[16,66,1]{1,0,2:T(8,128)S(1)} %copy.51), channel_id=1, source_target_pairs={{1,0},{3,2},{5,4},{7,6},{9,8},{11,10},{13,12},{15,14},{17,16},{19,... | collective-permute-start | bytes 12680 | tf_op jit(solution)/shard_map/ppermute | solution.py:23
  100.5 3.9 %collective-permute-start.23 = (f32[16,66,1]{1,0,2:T(8,128)S(1)}, f32[16,66,1]{1,0,2:T(8,128)S(1)}, u32[]{:S(2)}, u32[]{:S(2)}) collective-permute-start(f32[16,66,1]{1,0,2:T(8,128)S(1)} %copy.53), channel_id=1, source_target_pairs={{0,1},{2,3},{4,5},{6,7},{8,9},{10,11},{12,13},{14,15},{16,17},{18,... | collective-permute-start | bytes 12680 | tf_op jit(solution)/shard_map/ppermute | solution.py:21
  117.0 9.9 %copy-start.4 = (f32[16,64,512]{2,1,0:T(8,128)}, f32[16,64,512]{2,1,0:T(8,128)S(1)}, u32[]{:S(2)}) copy-start(f32[16,64,512]{2,1,0:T(8,128)S(1)} %get-tuple-element.8) | copy-start | bytes 6291460
  117.1 9.5 %collective-permute-start.26 = (f32[16,1,512]{2,0,1:T(8,128)S(1)}, f32[16,1,512]{2,0,1:T(8,128)S(1)}, u32[]{:S(2)}, u32[]{:S(2)}) collective-permute-start(f32[16,1,512]{2,0,1:T(8,128)S(1)} %copy.55), channel_id=1, source_target_pairs={{2,0},{4,2},{6,4},{3,1},{5,3},{7,5},{10,8},{12,10},{14,12},{11,9},... | collective-permute-start | bytes 98312 | tf_op jit(solution)/shard_map/ppermute | solution.py:23
  118.4 8.2 %collective-permute-start.27 = (f32[16,1,512]{2,0,1:T(8,128)S(1)}, f32[16,1,512]{2,0,1:T(8,128)S(1)}, u32[]{:S(2)}, u32[]{:S(2)}) collective-permute-start(f32[16,1,512]{2,0,1:T(8,128)S(1)} %copy.57), channel_id=1, source_target_pairs={{0,2},{2,4},{4,6},{1,3},{3,5},{5,7},{8,10},{10,12},{12,14},{9,11},... | collective-permute-start | bytes 98312 | tf_op jit(solution)/shard_map/ppermute | solution.py:21
  123.7 13.9 %collective-permute-start.24 = (f32[1,64,512]{2,1,0:T(8,128)}, f32[1,64,512]{2,1,0:T(8,128)S(1)}, u32[]{:S(2)}, u32[]{:S(2)}) collective-permute-start(f32[1,64,512]{2,1,0:T(8,128)} %get-tuple-element.26), channel_id=1, source_target_pairs={{8,0},{16,8},{24,16},{0,24},{9,1},{17,9},{25,17},{1,25},{10,2},{18... | collective-permute-start | bytes 393224 | tf_op jit(solution)/shard_map/ppermute | solution.py:23
  126.5 11.1 %collective-permute-start.25 = (f32[1,64,512]{2,1,0:T(8,128)}, f32[1,64,512]{2,1,0:T(8,128)}, u32[]{:S(2)}, u32[]{:S(2)}) collective-permute-start(f32[1,64,512]{2,1,0:T(8,128)} %get-tuple-element.27), channel_id=1, source_target_pairs={{0,8},{8,16},{16,24},{24,0},{1,9},{9,17},{17,25},{25,1},{2,10},{10... | collective-permute-start | bytes 393224 | tf_op jit(solution)/shard_map/ppermute | solution.py:21
  127.4 9.8 %collective-permute-start.29 = (f32[16,66,1]{1,0,2:T(8,128)S(1)}, f32[16,66,1]{1,0,2:T(8,128)S(1)}, u32[]{:S(2)}, u32[]{:S(2)}) collective-permute-start(f32[16,66,1]{1,0,2:T(8,128)S(1)} %copy.63), channel_id=1, source_target_pairs={{0,1},{2,3},{4,5},{6,7},{8,9},{10,11},{12,13},{14,15},{16,17},{18,... | collective-permute-start | bytes 12680 | tf_op jit(solution)/shard_map/ppermute | solution.py:21
  128.9 8.1 %collective-permute-start.28 = (f32[16,66,1]{1,0,2:T(8,128)S(1)}, f32[16,66,1]{1,0,2:T(8,128)S(1)}, u32[]{:S(2)}, u32[]{:S(2)}) collective-permute-start(f32[16,66,1]{1,0,2:T(8,128)S(1)} %copy.61), channel_id=1, source_target_pairs={{1,0},{3,2},{5,4},{7,6},{9,8},{11,10},{13,12},{15,14},{17,16},{19,... | collective-permute-start | bytes 12680 | tf_op jit(solution)/shard_map/ppermute | solution.py:23
where the time goes:
time: 194 us; the launch traced here: 193 us
  other arithmetic  71.9 us (37%)
  starting transfers between devices  64.6 us (33%)
  blocking collectives  41 us (21%)
  local copies, waits for them, and re-layouts  9.83 us (5%)
  between operations  3.02 us (2%)
  waiting for transfers between devices  2.65 us (1%)
    add x4, other arithmetic, local(): weights[iteration + 1] * weights[iteration] * direction  49.3 us
    psum x1, blocking collectives, local(): total = lax.psum(local_sum, ('gx', 'gy', 'gz'))  41 us
    ppermute x15, starting transfers between devices, padded(): lax.ppermute(tail, axis, [(i, (i + 1) % count) for i in range(ends)])  37.3 us
    ppermute x15, starting transfers between devices, padded(): lax.ppermute(head, axis, [((i + 1) % count, i) for i in range(ends)])  27.3 us
    reduce_sum x1, other arithmetic, local(): local_sum = jnp.sum(residual * residual)  12.5 us
    add x1, other arithmetic, local(): solution = solution + direction  6.8 us
    slice x15, local copies, waits for them, and re-layouts, padded(): head = lax.slice_in_dim(cells, 0, width, axis=dim)  4.85 us
  transfers between devices with their start and end apart: 30, of which 8 were waited for; matrix products, arithmetic and copies ran while one was open for 9% of the time, Pallas kernels for 0%

commit v1 on v0

v1 whole, which is shorter than its diff:
```python
import functools

import jax
import jax.numpy as jnp
from jax import lax
from jax.experimental import pallas as pl
from jax.experimental.pallas import tpu as pltpu
from jax.sharding import PartitionSpec as P

ITERS = 5
CHUNKS = 4
ROWS = 8

centre = 7.25
half_width = 6.75

AXES = ("gx", "gy", "gz")
PY, PZ = 8, 128
LOW, HIGH, INNER = 0, 1, 2


def chebyshev_weights(count):
    ratio_value = centre / half_width
    weights = [1.0 / ratio_value]
    for iteration in range(count):
        weights.append(1.0 / (2.0 * ratio_value - weights[-1]))
    return weights


def kernel(
    sizes,
    rhs,
    reaction,
    velocity,
    sol,
    res,
    norm,
    d,
    reac,
    vel,
    ysend,
    yrecv,
    part,
    load_sem,
    xs_sem,
    xr_sem,
    ys_sem,
    yr_sem,
    zs_sem,
    zr_sem,
    ps_sem,
    pr_sem,
):
    nx, ny, nz = rhs.shape
    weights = chebyshev_weights(ITERS)
    me = [lax.axis_index(a) for a in AXES]
    mid_y = pl.ds(PY, ny)
    mid_z = pl.ds(PZ, nz)
    chunk = ny // CHUNKS

    load_rhs = pltpu.make_async_copy(
        rhs, d.at[0, pl.ds(1, nx), mid_y, mid_z], load_sem.at[0]
    )
    load_rhs.start()
    loads = [pltpu.make_async_copy(reaction, reac, load_sem.at[1])] + [
        pltpu.make_async_copy(velocity.at[i], vel.at[i], load_sem.at[2 + i])
        for i in range(3)
    ]
    for copy in loads:
        copy.start()

    barrier = pltpu.get_barrier_semaphore()
    for a, n, i in zip(AXES, sizes, me):
        for p in range(1, n):
            pl.semaphore_signal(
                barrier,
                inc=1,
                device_id={a: lax.rem(i + p, n)},
                device_id_type=pl.DeviceIdType.MESH,
            )

    for side, at_edge in ((LOW, me[1] == 0), (HIGH, me[1] == sizes[1] - 1)):
        @pl.when(at_edge)
        def _(side=side):
            for slot in range(2):
                yrecv[slot, side] = jnp.zeros((nx, 1, nz), jnp.float32)

    for first, at_edge in ((0, me[2] == 0), (PZ + nz, me[2] == sizes[2] - 1)):
        @pl.when(at_edge)
        def _(first=first):
            def clear(x, carry):
                for slot in range(2):
                    d[slot, x, pl.ds(PY, ny), pl.ds(first, PZ)] = jnp.zeros(
                        (ny, PZ), jnp.float32
                    )
                return carry

            lax.fori_loop(1, nx + 1, clear, 0)

    pl.semaphore_wait(barrier, sum(n - 1 for n in sizes))

    def remote(src, dst, send, recv, axis, target):
        return pltpu.make_async_remote_copy(
            src_ref=src,
            dst_ref=dst,
            send_sem=send,
            recv_sem=recv,
            device_id={AXES[axis]: target},
            device_id_type=pl.DeviceIdType.MESH,
        )

    def x_copy(slot, side, c, source=None):
        n = sizes[0]
        rows = pl.ds(PY + c * chunk, chunk)
        plane, land, target = (
            (nx, 0, lax.rem(me[0] + 1, n))
            if side == LOW
            else (1, nx + 1, lax.rem(me[0] + n - 1, n))
        )
        if source is None:
            src = d.at[slot, plane, rows, mid_z]
        else:
            src = source.at[plane - 1, pl.ds(c * chunk, chunk), :]
        return remote(
            src,
            d.at[slot, land, rows, mid_z],
            xs_sem.at[slot, side, c],
            xr_sem.at[slot, side, c],
            0,
            target,
        )

    def span(group):
        return {LOW: (0, 1), HIGH: (nx - 1, 1), INNER: (1, nx - 2)}[group]

    def target_of(axis, side):
        n = sizes[axis]
        step = 1 if side == LOW else n - 1
        return lax.rem(me[axis] + step, n)

    def sends(axis, side):
        return me[axis] < sizes[axis] - 1 if side == LOW else me[axis] > 0

    def receives(axis, side):
        return me[axis] > 0 if side == LOW else me[axis] < sizes[axis] - 1

    def y_copy(slot, side, group):
        x = pl.ds(*span(group))
        return remote(
            ysend.at[slot, side, x],
            yrecv.at[slot, side, x],
            ys_sem.at[slot, side, group],
            yr_sem.at[slot, side, group],
            1,
            target_of(1, side),
        )

    def z_copy(slot, side, group):
        first, count = span(group)
        x = pl.ds(first + 1, count)
        source, land = (nz, 0) if side == LOW else (PZ, PZ + nz)
        return remote(
            d.at[slot, x, mid_y, pl.ds(source, PZ)],
            d.at[slot, x, mid_y, pl.ds(land, PZ)],
            zs_sem.at[slot, side, group],
            zr_sem.at[slot, side, group],
            2,
            target_of(2, side),
        )

    def open_each(slot, groups, act):
        for group in groups:
            for axis, copy in ((2, z_copy), (1, y_copy)):
                for side in (LOW, HIGH):
                    rule = receives if act == "wait_recv" else sends

                    @pl.when(rule(axis, side))
                    def _(copy=copy, side=side, group=group):
                        getattr(copy(slot, side, group), act)()

    def pack(slot, x):
        ysend[slot, LOW, x - 1] = d[slot, x, pl.ds(PY + ny - 1, 1), mid_z]
        ysend[slot, HIGH, x - 1] = d[slot, x, pl.ds(PY, 1), mid_z]

    def unpack(slot, x):
        d[slot, x, pl.ds(PY - 1, 1), mid_z] = yrecv[slot, LOW, x - 1]
        d[slot, x, pl.ds(PY + ny, 1), mid_z] = yrecv[slot, HIGH, x - 1]

    def block(k, x, y):
        slot, other = k % 2, (k + 1) % 2
        here = (x - 1, pl.ds(y, ROWS), slice(None))
        rows = pl.ds(PY + y, ROWS)
        mid = d[slot, x, rows, mid_z]
        px = d[slot, x + 1, rows, mid_z]
        mx = d[slot, x - 1, rows, mid_z]
        py = d[slot, x, pl.ds(PY + y + 1, ROWS), mid_z]
        my = d[slot, x, pl.ds(PY + y - 1, ROWS), mid_z]
        wide = nz + PZ
        pz = pltpu.roll(d[slot, x, rows, pl.ds(PZ, wide)], wide - 1, 1)[:, :nz]
        mz = pltpu.roll(d[slot, x, rows, pl.ds(0, wide)], 1, 1)[:, PZ:]
        beside = ((px + mx) + (py + my)) + (pz + mz)
        skew = vel[0, *here] * (px - mx) + vel[1, *here] * (py - my)
        skew = skew + vel[2, *here] * (pz - mz)
        applied = (6.0 + reac[here]) * mid - (beside - skew)
        if k == 0:
            left = mid - (1.0 / centre) * applied
            sol[here] = (1.0 / centre) * mid
        else:
            left = res[here] - applied
            sol[here] = sol[here] + mid
        res[here] = left
        if k + 1 < ITERS:
            keep = weights[k + 1] * weights[k] * (1.0 / centre if k == 0 else 1.0)
            d[other, x, rows, mid_z] = keep * mid + (
                2.0 * weights[k + 1] / half_width
            ) * left
            return None
        return left * left

    def add(total, term):
        return total if term is None else total + term

    for side in (LOW, HIGH):
        for c in range(CHUNKS):
            x_copy(0, side, c, rhs).start()
    load_rhs.wait()

    def pack_first(x, carry):
        pack(0, x)
        return carry

    lax.fori_loop(1, nx + 1, pack_first, 0)
    open_each(0, (INNER, LOW, HIGH), "start")
    for copy in loads:
        copy.wait()

    total = jnp.zeros((ROWS, nz), jnp.float32)
    for k in range(ITERS):
        slot, other = k % 2, (k + 1) % 2
        more = k + 1 < ITERS
        open_each(slot, (INNER,), "wait_recv")
        if k > 0:
            open_each(other, (INNER,), "wait_send")

        def inner(x, total, k=k, slot=slot, other=other, more=more):
            unpack(slot, x)
            for y in range(0, ny, ROWS):
                total = add(total, block(k, x, y))
            if more:
                pack(other, x)
            return total

        total = lax.fori_loop(2, nx, inner, total)
        if more:
            open_each(other, (INNER,), "start")
        open_each(slot, (LOW, HIGH), "wait_recv")
        if k > 0:
            open_each(other, (LOW, HIGH), "wait_send")
        unpack(slot, 1)
        unpack(slot, nx)
        for c in range(CHUNKS):
            for side in (LOW, HIGH):
                x_copy(slot, side, c).wait_recv()
                if k > 0:
                    x_copy(other, side, c, rhs if k == 1 else None).wait_send()
            for x in (1, nx):
                for y in range(c * chunk, (c + 1) * chunk, ROWS):
                    total = add(total, block(k, x, y))
            if more:
                for side in (LOW, HIGH):
                    x_copy(other, side, c).start()
        if more:
            pack(other, 1)
            pack(other, nx)
            open_each(other, (LOW, HIGH), "start")

    tile = total[:, :PZ]
    for z in range(PZ, nz, PZ):
        tile = tile + total[:, z : z + PZ]
    first = 0
    for axis in (2, 1, 0):
        n, i = sizes[axis], me[axis]
        part[first + i] = tile
        copies = [
            remote(
                part.at[first + i],
                part.at[first + i],
                ps_sem.at[first + p],
                pr_sem.at[first + p],
                axis,
                lax.rem(i + p, n),
            )
            for p in range(1, n)
        ]
        for copy in copies:
            copy.start()
        for copy in copies:
            copy.wait_recv()
        tile = part[first]
        for p in range(1, n):
            tile = tile + part[first + p]
        for copy in copies:
            copy.wait_send()
        first += n
    last = (ITERS - 1) % 2
    open_each(last, (INNER, LOW, HIGH), "wait_send")
    for c in range(CHUNKS):
        for side in (LOW, HIGH):
            x_copy(last, side, c).wait_send()
    cells = nx * ny * nz * sizes[0] * sizes[1] * sizes[2]
    mean = jnp.sum(tile, keepdims=True) / cells
    norm[...] = jnp.sqrt(mean + 1e-06)


def local(sizes, right_side, reaction, velocity):
    nx, ny, nz = right_side.shape
    hbm = pl.BlockSpec(memory_space=pltpu.HBM)
    vmem = pl.BlockSpec(memory_space=pltpu.VMEM)
    dma = pltpu.SemaphoreType.DMA
    field = jax.ShapeDtypeStruct((nx, ny, nz), jnp.float32)
    sol, res, norm = pl.pallas_call(
        functools.partial(kernel, sizes),
        out_shape=(field, field, jax.ShapeDtypeStruct((1, 1), jnp.float32)),
        in_specs=[hbm] * 3,
        out_specs=(vmem, vmem, vmem),
        scratch_shapes=[
            pltpu.VMEM((2, nx + 2, ny + 2 * PY, nz + 2 * PZ), jnp.float32),
            pltpu.VMEM((nx, ny, nz), jnp.float32),
            pltpu.VMEM((3, nx, ny, nz), jnp.float32),
            pltpu.VMEM((2, 2, nx, 1, nz), jnp.float32),
            pltpu.VMEM((2, 2, nx, 1, nz), jnp.float32),
            pltpu.VMEM((sum(sizes), ROWS, PZ), jnp.float32),
            dma((5,)),
            dma((2, 2, CHUNKS)),
            dma((2, 2, CHUNKS)),
            dma((2, 2, 3)),
            dma((2, 2, 3)),
            dma((2, 2, 3)),
            dma((2, 2, 3)),
            dma((sum(sizes),)),
            dma((sum(sizes),)),
        ],
        compiler_params=pltpu.CompilerParams(
            collective_id=0,
            has_side_effects=True,
            vmem_limit_bytes=40 * 1024 * 1024,
        ),
    )(right_side, reaction, velocity)
    return sol, res, norm[0, 0]


def solution(mesh):
    sizes = tuple(mesh.shape[a] for a in AXES)
    return jax.shard_map(
        functools.partial(local, sizes),
        mesh=mesh,
        in_specs=(P("gx", "gy", "gz"), P("gx", "gy", "gz"), P(None, "gx", "gy", "gz")),
        out_specs=(P("gx", "gy", "gz"), P("gx", "gy", "gz"), P()),
        check_vma=False,
    )
```

time: 194 us -> 53.6 us (0.28)
  other arithmetic: 71.9 us -> 0 us
  starting transfers between devices: 64.6 us -> 0 us
  Pallas kernels: 0 us -> 45.2 us
  blocking collectives: 41 us -> 0 us
  local copies, waits for them, and re-layouts: 9.83 us -> 5.81 us
  waiting for transfers between devices: 2.65 us -> 0 us
    ppermute x30 -> x0, starting transfers between devices: 64.6 us -> none  [the longest x15 37.3 us: padded(): lax.ppermute(tail, axis, [(i, (i + 1) % count) for i in range(ends)])]
    add x5 -> x0, other arithmetic: 56.1 us -> none  [the longest x4 49.3 us: local(): weights[iteration + 1] * weights[iteration] * direction]
    pallas_call x0 -> x1, Pallas kernels: none -> 45.2 us  [local(): pl.pallas_call(functools.partial(kernel, sizes), out_shape=(field, field,...]
    psum x1 -> x0, blocking collectives: 41 us -> none  [local(): total = lax.psum(local_sum, ('gx', 'gy', 'gz'))]
    reduce_sum x1 -> x0, other arithmetic: 12.5 us -> none  [local(): local_sum = jnp.sum(residual * residual)]
    slice x30 -> x0, local copies, waits for them, and re-layouts: 6.35 us -> none  [the longest x15 4.85 us: padded(): head = lax.slice_in_dim(cells, 0, width, axis=dim)]
    unnamed x12 -> x6, local copies, waits for them, and re-layouts: 0.03 us -> 5.81 us
    ppermute x20 -> x0, local copies, waits for them, and re-layouts: 3.45 us -> none  [the longest x10 1.73 us: padded(): lax.ppermute(tail, axis, [(i, (i + 1) % count) for i in range(ends)])]
  transfers between devices with their start and end apart: 30 -> 0, of which waited for: 8 -> 0; matrix products, arithmetic and copies ran while one was open for 9% -> 0% of each run, Pallas kernels for 0% -> 0%
where the time goes in v1:
time: 53.6 us; the launch traced here: 53.4 us
  Pallas kernels  45.2 us (84%)
  local copies, waits for them, and re-layouts  5.81 us (11%)
  between operations  2.41 us (4%)
    pallas_call x1, Pallas kernels, local(): pl.pallas_call(functools.partial(kernel, sizes), out_shape=(field, field,...  45.2 us
    unnamed x6, local copies, waits for them, and re-layouts  5.81 us

profile of v1, /device:TPU:0, one launch (start us, length us, event | category | flops | bytes accessed | tf_op | source)
XLA Modules:
  0.0 53.4 jit_solution(3640415721401158456)
XLA Ops:
  0.6 0.0 copy-start
  0.6 1.6 %copy-done = f32[16,64,512]{2,1,0:T(8,128)S(1)} copy-done((f32[16,64,512]{2,1,0:T(8,128)S(1)}, f32[16,64,512]{2,1,0:T(8,128)}, u32[]{:S(2)}) %copy-start) | copy-done | bytes 2097176
  2.2 0.0 copy-start.1
  2.2 1.6 %copy-done.1 = f32[16,64,512]{2,1,0:T(8,128)S(1)} copy-done((f32[16,64,512]{2,1,0:T(8,128)S(1)}, f32[16,64,512]{2,1,0:T(8,128)}, u32[]{:S(2)}) %copy-start.1) | copy-done | bytes 2097176
  3.8 45.2 %shard_map.58 = (f32[16,64,512]{2,1,0:T(8,128)S(1)}, f32[16,64,512]{2,1,0:T(8,128)S(1)}, f32[1,1]{1,0:T(1,128)}) custom-call(f32[16,64,512]{2,1,0:T(8,128)S(1)} %copy-done, f32[16,64,512]{2,1,0:T(8,128)S(1)} %copy-done.1, f32[3,16,64,512]{3,2,1,0:T(8,128)} %velocity.1), custom_call_target="tpu_custom_call" | custom-call | tf_op jit(solution)/shard_map/pallas_call | solution.py:321
  49.0 1.3 %copy.9 = f32[16,64,512]{2,1,0:T(8,128)} copy(f32[16,64,512]{2,1,0:T(8,128)S(1)} %get-tuple-element.12) | data formatting | bytes 4194304
  50.4 1.3 %copy.10 = f32[16,64,512]{2,1,0:T(8,128)} copy(f32[16,64,512]{2,1,0:T(8,128)S(1)} %get-tuple-element.13) | data formatting | bytes 4194304
Async XLA Ops:
  0.6 1.6 %copy-start = (f32[16,64,512]{2,1,0:T(8,128)S(1)}, f32[16,64,512]{2,1,0:T(8,128)}, u32[]{:S(2)}) copy-start(f32[16,64,512]{2,1,0:T(8,128)} %rhs.1) | copy-start | bytes 6291460
  2.2 1.6 %copy-start.1 = (f32[16,64,512]{2,1,0:T(8,128)S(1)}, f32[16,64,512]{2,1,0:T(8,128)}, u32[]{:S(2)}) copy-start(f32[16,64,512]{2,1,0:T(8,128)} %reaction.1) | copy-start | bytes 6291460

commit v2 on v1

--- a/solution.py
+++ b/solution.py
@@ -1,4 +1,5 @@
 import functools
+import itertools
 
 import jax
 import jax.numpy as jnp
@@ -25,6 +26,25 @@
     for iteration in range(count):
         weights.append(1.0 / (2.0 * ratio_value - weights[-1]))
     return weights
+
+
+PHASES = ((2,), (0, 1))
+
+
+def phase_steps(sizes, axes):
+    ranges = [range(n) if i in axes else (0,) for i, n in enumerate(sizes)]
+    return [steps for steps in itertools.product(*ranges) if any(steps)]
+
+
+def greeted_by(sizes):
+    steps = set()
+    for axes in PHASES:
+        steps |= set(phase_steps(sizes, axes))
+    return sorted(steps)
+
+
+def phase_slots(sizes):
+    return sum(len(phase_steps(sizes, axes)) + 1 for axes in PHASES)
 
 
 def kernel(
@@ -70,14 +90,21 @@
         copy.start()
 
     barrier = pltpu.get_barrier_semaphore()
-    for a, n, i in zip(AXES, sizes, me):
-        for p in range(1, n):
-            pl.semaphore_signal(
-                barrier,
-                inc=1,
-                device_id={a: lax.rem(i + p, n)},
-                device_id_type=pl.DeviceIdType.MESH,
-            )
+    def shifted(steps):
+        return {
+            a: lax.rem(i + p, n)
+            for a, n, i, p in zip(AXES, sizes, me, steps)
+            if p
+        }
+
+    greeted = greeted_by(sizes)
+    for steps in greeted:
+        pl.semaphore_signal(
+            barrier,
+            inc=1,
+            device_id=shifted(steps),
+            device_id_type=pl.DeviceIdType.MESH,
+        )
 
     for side, at_edge in ((LOW, me[1] == 0), (HIGH, me[1] == sizes[1] - 1)):
         @pl.when(at_edge)
@@ -97,7 +124,7 @@
 
             lax.fori_loop(1, nx + 1, clear, 0)
 
-    pl.semaphore_wait(barrier, sum(n - 1 for n in sizes))
+    pl.semaphore_wait(barrier, len(greeted))
 
     def remote(src, dst, send, recv, axis, target):
         return pltpu.make_async_remote_copy(
@@ -278,30 +305,33 @@
     for z in range(PZ, nz, PZ):
         tile = tile + total[:, z : z + PZ]
     first = 0
-    for axis in (2, 1, 0):
-        n, i = sizes[axis], me[axis]
-        part[first + i] = tile
+    for axes in PHASES:
+        group = phase_steps(sizes, axes)
+        own = jnp.int32(0)
+        for axis in axes:
+            own = own * sizes[axis] + me[axis]
+        part[first + own] = tile
         copies = [
-            remote(
-                part.at[first + i],
-                part.at[first + i],
-                ps_sem.at[first + p],
-                pr_sem.at[first + p],
-                axis,
-                lax.rem(i + p, n),
+            pltpu.make_async_remote_copy(
+                src_ref=part.at[first + own],
+                dst_ref=part.at[first + own],
+                send_sem=ps_sem.at[first + p],
+                recv_sem=pr_sem.at[first + p],
+                device_id=shifted(steps),
+                device_id_type=pl.DeviceIdType.MESH,
             )
-            for p in range(1, n)
+            for p, steps in enumerate(group)
         ]
         for copy in copies:
             copy.start()
         for copy in copies:
             copy.wait_recv()
         tile = part[first]
-        for p in range(1, n):
+        for p in range(1, len(group) + 1):
             tile = tile + part[first + p]
         for copy in copies:
             copy.wait_send()
-        first += n
+        first += len(group) + 1
     last = (ITERS - 1) % 2
     open_each(last, (INNER, LOW, HIGH), "wait_send")
     for c in range(CHUNKS):
@@ -329,7 +359,7 @@
             pltpu.VMEM((3, nx, ny, nz), jnp.float32),
             pltpu.VMEM((2, 2, nx, 1, nz), jnp.float32),
             pltpu.VMEM((2, 2, nx, 1, nz), jnp.float32),
-            pltpu.VMEM((sum(sizes), ROWS, PZ), jnp.float32),
+            pltpu.VMEM((phase_slots(sizes), ROWS, PZ), jnp.float32),
             dma((5,)),
             dma((2, 2, CHUNKS)),
             dma((2, 2, CHUNKS)),
@@ -337,15 +367,20 @@
             dma((2, 2, 3)),
             dma((2, 2, 3)),
             dma((2, 2, 3)),
-            dma((sum(sizes),)),
-            dma((sum(sizes),)),
+            dma((phase_slots(sizes),)),
+            dma((phase_slots(sizes),)),
         ],
         compiler_params=pltpu.CompilerParams(
             collective_id=0,
             has_side_effects=True,
             vmem_limit_bytes=40 * 1024 * 1024,
         ),
-    )(right_side, reaction, velocity)
+    )(
+        *(
+            pltpu.with_memory_space_constraint(a, pltpu.HBM)
+            for a in (right_side, reaction, velocity)
+        )
+    )
     return sol, res, norm[0, 0]
 
 

time: 53.6 us -> 49.7 us (0.927)
  local copies, waits for them, and re-layouts: 5.81 us -> 2.64 us
  Pallas kernels: 45.2 us -> 44.6 us
    unnamed x6 -> x2, local copies, waits for them, and re-layouts: 5.81 us -> 2.64 us
    pallas_call x1, Pallas kernels: 45.2 us -> 44.6 us  [local(): pl.pallas_call(functools.partial(kernel, sizes), out_shape=(field, field,...]
where the time goes in v2:
time: 49.7 us; the launch traced here: 49.6 us
  Pallas kernels  44.6 us (90%)
  local copies, waits for them, and re-layouts  2.64 us (5%)
  between operations  2.33 us (5%)
    pallas_call x1, Pallas kernels, local(): pl.pallas_call(functools.partial(kernel, sizes), out_shape=(field, field,...  44.6 us
    unnamed x2, local copies, waits for them, and re-layouts  2.64 us

profile of v2, /device:TPU:0, one launch (start us, length us, event | category | flops | bytes accessed | tf_op | source)
XLA Modules:
  0.0 49.6 jit_solution(8327966194331353436)
XLA Ops:
  0.6 44.6 %shard_map.58 = (f32[16,64,512]{2,1,0:T(8,128)S(1)}, f32[16,64,512]{2,1,0:T(8,128)S(1)}, f32[1,1]{1,0:T(1,128)}) custom-call(f32[16,64,512]{2,1,0:T(8,128)} %rhs.1, f32[16,64,512]{2,1,0:T(8,128)} %reaction.1, f32[3,16,64,512]{3,2,1,0:T(8,128)} %velocity.1), custom_call_target="tpu_custom_call" | custom-call | tf_op jit(solution)/shard_map/pallas_call | solution.py:351
  45.2 1.3 %copy.9 = f32[16,64,512]{2,1,0:T(8,128)} copy(f32[16,64,512]{2,1,0:T(8,128)S(1)} %get-tuple-element.12) | data formatting | bytes 4194304
  46.6 1.3 %copy.10 = f32[16,64,512]{2,1,0:T(8,128)} copy(f32[16,64,512]{2,1,0:T(8,128)S(1)} %get-tuple-element.13) | data formatting | bytes 4194304

commit v3 on v2

--- a/solution.py
+++ b/solution.py
@@ -37,7 +37,13 @@
 
 
 def greeted_by(sizes):
-    steps = set()
+    steps = {
+        tuple(p if j == i else 0 for j in range(len(sizes)))
+        for i, n in enumerate(sizes)
+        for p in (1, n - 1)
+    }
+    if sizes[0] // 2 + sizes[1] - 1 + sizes[2] - 1 <= ITERS + 1:
+        return sorted(steps)
     for axes in PHASES:
         steps |= set(phase_steps(sizes, axes))
     return sorted(steps)

time: 49.7 us -> 48.4 us (0.974)
  Pallas kernels: 44.6 us -> 43.3 us
    pallas_call x1, Pallas kernels: 44.6 us -> 43.3 us  [local(): pl.pallas_call(functools.partial(kernel, sizes), out_shape=(field, field,...]
where the time goes in v3:
time: 48.4 us; the launch traced here: 48.2 us
  Pallas kernels  43.3 us (89%)
  local copies, waits for them, and re-layouts  2.64 us (5%)
  between operations  2.33 us (5%)
    pallas_call x1, Pallas kernels, local(): pl.pallas_call(functools.partial(kernel, sizes), out_shape=(field, field,...  43.3 us
    unnamed x2, local copies, waits for them, and re-layouts  2.64 us

profile of v3, /device:TPU:0, one launch (start us, length us, event | category | flops | bytes accessed | tf_op | source)
XLA Modules:
  0.0 48.2 jit_solution(17478560248621485291)
XLA Ops:
  0.6 43.3 %shard_map.58 = (f32[16,64,512]{2,1,0:T(8,128)S(1)}, f32[16,64,512]{2,1,0:T(8,128)S(1)}, f32[1,1]{1,0:T(1,128)}) custom-call(f32[16,64,512]{2,1,0:T(8,128)} %rhs.1, f32[16,64,512]{2,1,0:T(8,128)} %reaction.1, f32[3,16,64,512]{3,2,1,0:T(8,128)} %velocity.1), custom_call_target="tpu_custom_call" | custom-call | tf_op jit(solution)/shard_map/pallas_call | solution.py:357
  43.9 1.3 %copy.9 = f32[16,64,512]{2,1,0:T(8,128)} copy(f32[16,64,512]{2,1,0:T(8,128)S(1)} %get-tuple-element.12) | data formatting | bytes 4194304
  45.2 1.3 %copy.10 = f32[16,64,512]{2,1,0:T(8,128)} copy(f32[16,64,512]{2,1,0:T(8,128)S(1)} %get-tuple-element.13) | data formatting | bytes 4194304
